TPU v7x, 256 devices: a whole 4x4x8 slice. The times are simulated.
256 devices in a mesh: loc: 32 (over y, x, core), tm: 8 (over z).
Axes of the slice: x: 4, y: 4, z: 8, core: 2. Of those that a mesh axis runs over, the one named last changes fastest.
Arguments:
- observed: float32 [4096, 1024], P('loc', 'tm'), may hold values from -6 to 6
- observed_mask: int32 [4096, 1024], P('loc', 'tm'), may hold values 0 or 1
- training_site_positions: float32 [2, 4096], replicated, may hold values from 0 to 1
- time_stamps: float32 [1024], replicated, may hold values from 0 to 1
- noise_var: float32 [1024], P('tm'), may hold values from 0.2 to 2
- test_coords: float32 [2, 4096], replicated, may hold values from 0 to 1
- site_order: int32 [4096], replicated, may hold values from 0 to 4095, each once
Outputs:
- solver_estimate: float32 [4096, 1024], P('loc', 'tm')
- posterior_mean_field: float32 [4096, 1024], P('loc', 'tm')
Inputs may be any that keep to these rules, and one draw needn't show every extreme that they name: `site_order`: each test site appears once.
All inputs are finite; a program needn't handle non-finite values. No bound on the sum of `observed_mask` on one device may be relied on, other than what follows from the above.
Results may differ from a plain program's by a relative error of at most 0.00022.
Values sent between devices are 32-bit elements; how exact they have to be, the bound alone decides.
No kernel may reach another device: no remote copies, remote signals or barrier semaphores. Data moves between devices by JAX's collectives and lax.ppermute only.
A program may use at most 64 MiB of HBM per device.

v0:
```python
import math
import jax
import jax.numpy as jnp
from jax import lax
from jax.sharding import Mesh
from jax.sharding import PartitionSpec as P

ITERS = 2
LOC = ("loc_0", "loc_1", "loc_2")
LOC_TM = ("loc_0", "loc_1", "loc_2", "tm")
root_three = math.sqrt(3.0)
space_reach = 2.5
time_reach = 5.0
covariance_times_iterate = 0.1


def from_everyone(shard, axis):
    copies = jnp.broadcast_to(shard, (lax.axis_size(axis), *shard.shape))
    return lax.all_to_all(copies, axis, split_axis=0, concat_axis=0, tiled=True)


def in_order(parts, dim):
    parts = jnp.moveaxis(parts, 0, dim)
    shape = parts.shape
    return parts.reshape(*shape[:dim], shape[dim] * shape[dim + 1], *shape[dim + 2 :])


def collect(shard, axis, dim):
    parts = from_everyone(shard, axis)
    return in_order(parts, dim)


def by_axis(shard, axes):
    for axis in axes:
        shard = lax.psum(shard, axis)
    return shard


def split_up(shard, dim, length):
    shape = shard.shape
    parts = shard.reshape(*shape[:dim], length, shape[dim] // length, *shape[dim + 1 :])
    return jnp.moveaxis(parts, dim, 0)


def summed_on_arrival(shard, axis, dim):
    parts = split_up(shard, dim, lax.axis_size(axis))
    arrived = lax.all_to_all(parts, axis, split_axis=0, concat_axis=0, tiled=True)
    return arrived.sum(axis=0)


def matern(left_points, right_points, length):
    squared = jnp.sum(jnp.square(left_points[:, :, None] - right_points[:, None, :]), axis=0)
    scaled = jnp.sqrt(squared) * (root_three / length)
    return (1.0 + scaled) * jnp.exp(-scaled)


def between_covariance_block(row_points, col_points, right_side, length):
    row_count = row_points.shape[1]
    block_size = math.gcd(row_count, 2048)
    number = row_count // block_size
    blocks = row_points.reshape(row_points.shape[0], number, block_size).transpose(1, 0, 2)

    def one_block(points):
        return jnp.dot(
            matern(points, col_points, length),
            right_side,
            precision=lax.Precision.HIGHEST,
            preferred_element_type=jnp.float32,
        )

    return lax.map(one_block, blocks).reshape(row_count, right_side.shape[1])


def column_sum(row_points, col_points, right_side, length):
    col_count = col_points.shape[1]
    block_size = math.gcd(col_count, 2048)
    number = col_count // block_size

    def add_block(index, summed):
        offset = index * block_size
        columns = lax.dynamic_slice_in_dim(col_points, offset, block_size, 1)
        rows_part = lax.dynamic_slice_in_dim(right_side, offset, block_size, 0)
        kernel = matern(row_points, columns, length)
        return summed + jnp.dot(
            kernel, rows_part, precision=lax.Precision.HIGHEST, preferred_element_type=jnp.float32
        )

    empty = jnp.zeros((row_points.shape[1], right_side.shape[1]), jnp.float32)
    return lax.fori_loop(0, number, add_block, empty)


def on_device(
    observed,
    observed_mask,
    training_site_positions,
    time_stamps,
    noise_var,
    test_coords,
    site_order,
):
    loc_rows = observed.shape[0]
    time_cols = observed.shape[1]
    mask_float = observed_mask.astype(jnp.float32)
    planar_correlation_range = space_reach / math.sqrt(training_site_positions.shape[1])
    time_length = time_reach / time_stamps.shape[0]
    own_points = lax.dynamic_slice_in_dim(
        training_site_positions, lax.axis_index(LOC) * loc_rows, loc_rows, 1
    )
    own_stamps = lax.dynamic_slice_in_dim(
        time_stamps, lax.axis_index("tm") * time_cols, time_cols, 0
    )

    def time_fold(shard_piece):
        kernel = matern(time_stamps[None, :], own_stamps[None, :], time_length)
        return jnp.dot(
            shard_piece, kernel, precision=lax.Precision.HIGHEST, preferred_element_type=jnp.float32
        )

    def squares(residual):
        return by_axis(jnp.sum(residual * residual), LOC_TM)

    solver_estimate = jnp.zeros_like(observed)
    residual = mask_float * observed
    direction = residual
    norm_now = squares(residual)
    for iteration in range(ITERS):
        masked = mask_float * direction
        inner = time_fold(collect(masked, "tm", 1))
        outer = column_sum(
            own_points, training_site_positions, collect(inner, LOC, 0), planar_correlation_range
        )
        image = mask_float * outer * covariance_times_iterate + direction * noise_var[None, :]
        curvature_sum = by_axis(jnp.sum(direction * image), LOC_TM)
        step_size = norm_now / curvature_sum
        solver_estimate = solver_estimate + step_size * direction
        residual = residual - step_size * image
        if iteration + 1 < ITERS:
            norm_next = squares(residual)
            direction = residual + norm_next / norm_now * direction
            norm_now = norm_next
    temporal_observation_grid = time_fold(collect(solver_estimate, "tm", 1))
    unseen_site_positions = test_coords[:, site_order]
    local_share = summed_on_arrival(
        between_covariance_block(
            unseen_site_positions, own_points, temporal_observation_grid, planar_correlation_range
        ),
        LOC,
        0,
    )
    posterior_mean_field = local_share * covariance_times_iterate
    return (solver_estimate, posterior_mean_field)


def solution(mesh):
    split = Mesh(mesh.devices.reshape(4, 4, 2, mesh.shape["tm"]), ("loc_0", "loc_1", "loc_2", "tm"))
    in_specs = (P(LOC, "tm"), P(LOC, "tm"), P(), P(), P("tm"), P(), P())
    out_specs = (P(LOC, "tm"), P(LOC, "tm"))
    return jax.shard_map(
        on_device, mesh=split, in_specs=in_specs, out_specs=out_specs, check_vma=False
    )
```

profile of v0, /device:TPU:1, one launch (start us, length us, event | category | flops | bytes accessed | tf_op | source)
XLA Modules:
  0.0 312.8 jit_solution(4415096766362854588)
XLA Ops:
  2.4 9.0 %all-to-all-start = ((f32[8,128,128]{1,2,0:T(8,128)}), f32[8,128,128]{1,2,0:T(8,128)S(1)}, u32[]{:S(2)}, u32[]{:S(2)}) async-start(f32[8,128,128]{1,2,0:T(8,128)} %broadcast_in_dim.41), calls=%async_computation | async-start | bytes 1048576 | tf_op jit(solution)/shard_map/all_to_all | solution.py:19
  12.2 17.2 %all-to-all-done = f32[8,128,128]{1,2,0:T(8,128)S(1)} async-done(((f32[8,128,128]{1,2,0:T(8,128)}), f32[8,128,128]{1,2,0:T(8,128)S(1)}, u32[]{:S(2)}, u32[]{:S(2)}) %all-to-all-start) | async-done | bytes 524320 | tf_op jit(solution)/shard_map/all_to_all | solution.py:19
  32.9 7.7 %all-to-all-start.1 = ((f32[32,128,128]{2,1,0:T(8,128)}), f32[32,128,128]{2,1,0:T(8,128)S(1)}, u32[]{:S(2)}, u32[]{:S(2)}) async-start(f32[32,128,128]{2,1,0:T(8,128)} %broadcast_in_dim.42), calls=%async_computation.1 | async-start | bytes 4194304 | tf_op jit(solution)/shard_map/all_to_all | solution.py:19
  40.7 28.5 %all-to-all-done.1 = f32[32,128,128]{2,1,0:T(8,128)S(1)} async-done(((f32[32,128,128]{2,1,0:T(8,128)}), f32[32,128,128]{2,1,0:T(8,128)S(1)}, u32[]{:S(2)}, u32[]{:S(2)}) %all-to-all-start.1) | async-done | bytes 2097184 | tf_op jit(solution)/shard_map/all_to_all | solution.py:19
  69.2 3.7 %while.39 = (s32[]{:T(128)}, f32[128,128]{1,0:T(8,128)S(1)}, f32[2,128]{1,0:T(2,128)S(1)}, f32[2,4096]{1,0:T(2,128)S(1)}, f32[4096,128]{1,0:T(8,128)S(1)}, /*index=5*/s32[]{:T(128)}, s32[]{:T(128)}, s32[]{:T(128)}, s32[]{:T(128)}) while((s32[]{:T(128)}, f32[128,128]{1,0:T(8,128)S(1)}, f32[2,128]{1,0:T(2,128)S(1)}, ...), condition=%wide.region_7.8_spmd.clone, body=%wide.region_5.7_spmd.clone.sunk | while | flops 405045248 | bytes 3327133 | solution.py:89
  73.6 6.7 %all-reduce.2 = (f32[]{:T(128)}, f32[]{:T(128)}) all-reduce(f32[]{:T(128)} %get-tuple-element.257, f32[]{:T(128)} %get-tuple-element.256), channel_id=1, replica_groups=mesh['loc_0'=4,'loc_1'=4,'loc_2'=2,'tm'=8] {'loc_0'}, use_global_device_ids=true, to_apply=%region_1.0 | all-reduce | flops 2 | bytes 16 | tf_op jit(solution)/shard_map/psum | solution.py:35
  80.4 9.8 %all-reduce.1 = (f32[]{:T(128)}, f32[]{:T(128)}) all-reduce(f32[]{:T(128)} %get-tuple-element.292, f32[]{:T(128)} %get-tuple-element.293), channel_id=1, replica_groups=mesh['loc_0'=4,'loc_1'=4,'loc_2'=2,'tm'=8] {'loc_1'}, use_global_device_ids=true, to_apply=%region_2.0 | all-reduce | flops 2 | bytes 16 | tf_op jit(solution)/shard_map/psum | solution.py:35
  90.2 5.9 %all-reduce.3 = (f32[]{:T(128)}, f32[]{:T(128)}) all-reduce(f32[]{:T(128)} %get-tuple-element.290, f32[]{:T(128)} %get-tuple-element.291), channel_id=1, replica_groups=mesh['loc_0'=4,'loc_1'=4,'loc_2'=2,'tm'=8] {'loc_2'}, use_global_device_ids=true, to_apply=%region_3.0 | all-reduce | flops 2 | bytes 16 | tf_op jit(solution)/shard_map/psum | solution.py:35
  96.1 11.6 %all-reduce = (f32[]{:T(128)}, f32[]{:T(128)}) all-reduce(f32[]{:T(128)} %get-tuple-element.294, f32[]{:T(128)} %get-tuple-element.295), channel_id=1, replica_groups=mesh['loc_0'=4,'loc_1'=4,'loc_2'=2,'tm'=8] {'tm'}, use_global_device_ids=true, to_apply=%region_4.0 | all-reduce | flops 2 | bytes 16 | tf_op jit(solution)/shard_map/psum | solution.py:35
  109.6 7.2 %psum.120 = f32[]{:T(128)} all-reduce(f32[]{:T(128)} %multiply_reduce_fusion.4), channel_id=1, replica_groups=mesh['loc_0'=4,'loc_1'=4,'loc_2'=2,'tm'=8] {'loc_0'}, use_global_device_ids=true, to_apply=%region_14.0 | all-reduce | flops 1 | bytes 8 | tf_op jit(solution)/shard_map/psum | solution.py:35
  116.7 8.4 %psum.121 = f32[]{:T(128)} all-reduce(f32[]{:T(128)} %psum.120), channel_id=1, replica_groups=mesh['loc_0'=4,'loc_1'=4,'loc_2'=2,'tm'=8] {'loc_1'}, use_global_device_ids=true, to_apply=%region_15.0 | all-reduce | flops 1 | bytes 8 | tf_op jit(solution)/shard_map/psum | solution.py:35
  125.2 10.8 %psum.122 = f32[]{:T(128)} all-reduce(f32[]{:T(128)} %psum.121), channel_id=1, replica_groups=mesh['loc_0'=4,'loc_1'=4,'loc_2'=2,'tm'=8] {'loc_2'}, use_global_device_ids=true, to_apply=%region_16.0 | all-reduce | flops 1 | bytes 8 | tf_op jit(solution)/shard_map/psum | solution.py:35
  135.9 12.5 %psum.123 = f32[]{:T(128)} all-reduce(f32[]{:T(128)} %psum.122), channel_id=1, replica_groups=mesh['loc_0'=4,'loc_1'=4,'loc_2'=2,'tm'=8] {'tm'}, use_global_device_ids=true, to_apply=%region_17.0 | all-reduce | flops 1 | bytes 8 | tf_op jit(solution)/shard_map/psum | solution.py:35
  149.8 16.1 %all_to_all.30 = f32[8,128,128]{1,2,0:T(8,128)S(1)} all-to-all(f32[8,128,128]{1,2,0:T(8,128)S(1)} %broadcast_in_dim.43), channel_id=1, replica_groups=mesh['loc_0'=4,'loc_1'=4,'loc_2'=2,'tm'=8] {'tm'}, dimensions={0} | all-to-all | bytes 1048576 | tf_op jit(solution)/shard_map/all_to_all | solution.py:19
  168.8 9.2 %all-to-all-start.3 = ((f32[32,128,128]{2,1,0:T(8,128)}), f32[32,128,128]{2,1,0:T(8,128)S(1)}, u32[]{:S(2)}, u32[]{:S(2)}) async-start(f32[32,128,128]{2,1,0:T(8,128)} %broadcast_in_dim.44), calls=%async_computation.3 | async-start | bytes 4194304 | tf_op jit(solution)/shard_map/all_to_all | solution.py:19
  177.9 28.3 %all-to-all-done.3 = f32[32,128,128]{2,1,0:T(8,128)S(1)} async-done(((f32[32,128,128]{2,1,0:T(8,128)}), f32[32,128,128]{2,1,0:T(8,128)S(1)}, u32[]{:S(2)}, u32[]{:S(2)}) %all-to-all-start.3) | async-done | bytes 2097184 | tf_op jit(solution)/shard_map/all_to_all | solution.py:19
  206.2 3.7 %while.40 = (s32[]{:T(128)}, f32[128,128]{1,0:T(8,128)S(1)}, f32[2,128]{1,0:T(2,128)S(1)}, f32[2,4096]{1,0:T(2,128)S(1)}, f32[4096,128]{1,0:T(8,128)S(1)}, /*index=5*/s32[]{:T(128)}, s32[]{:T(128)}, s32[]{:T(128)}, s32[]{:T(128)}) while((s32[]{:T(128)}, f32[128,128]{1,0:T(8,128)S(1)}, f32[2,128]{1,0:T(2,128)S(1)}, ...), condition=%wide.region_20.21_spmd.clone, body=%wide.region_18.20_spmd.clone.sunk | while | flops 405045248 | bytes 3327133 | solution.py:89
  210.7 7.0 %psum.124 = f32[]{:T(128)} all-reduce(f32[]{:T(128)} %multiply_reduce_fusion.3), channel_id=1, replica_groups=mesh['loc_0'=4,'loc_1'=4,'loc_2'=2,'tm'=8] {'loc_0'}, use_global_device_ids=true, to_apply=%region_22.0 | all-reduce | flops 1 | bytes 8 | tf_op jit(solution)/shard_map/psum | solution.py:35
  217.7 10.0 %psum.125 = f32[]{:T(128)} all-reduce(f32[]{:T(128)} %psum.124), channel_id=1, replica_groups=mesh['loc_0'=4,'loc_1'=4,'loc_2'=2,'tm'=8] {'loc_1'}, use_global_device_ids=true, to_apply=%region_23.0 | all-reduce | flops 1 | bytes 8 | tf_op jit(solution)/shard_map/psum | solution.py:35
  227.7 6.0 %psum.126 = f32[]{:T(128)} all-reduce(f32[]{:T(128)} %psum.125), channel_id=1, replica_groups=mesh['loc_0'=4,'loc_1'=4,'loc_2'=2,'tm'=8] {'loc_2'}, use_global_device_ids=true, to_apply=%region_24.0 | all-reduce | flops 1 | bytes 8 | tf_op jit(solution)/shard_map/psum | solution.py:35
  233.7 11.6 %psum.127 = f32[]{:T(128)} all-reduce(f32[]{:T(128)} %psum.126), channel_id=1, replica_groups=mesh['loc_0'=4,'loc_1'=4,'loc_2'=2,'tm'=8] {'tm'}, use_global_device_ids=true, to_apply=%region_25.0 | all-reduce | flops 1 | bytes 8 | tf_op jit(solution)/shard_map/psum | solution.py:35
  252.1 14.1 %gather_fusion = f32[4096,2]{1,0:T(8,128)} fusion(f32[2,4096]{0,1:T(8,128)S(1)} %copy.23, s32[4096]{0:T(1024)S(1)} %fusion.53), kind=kCustom, calls=%fused_computation | custom fusion | bytes 81920 | tf_op jit(solution)/shard_map/gather | solution.py:142
  269.6 6.2 %while.38 = (s32[]{:T(128)}, f32[2,2048,128]{2,1,0:T(8,128)}, f32[2,2,2048]{2,1,0:T(2,128)S(1)}, f32[2,128]{1,0:T(2,128)S(1)}, f32[128,128]{1,0:T(8,128)S(1)}, /*index=5*/s32[]{:T(128)}) while((s32[]{:T(128)}, f32[2,2048,128]{2,1,0:T(8,128)}, f32[2,2,2048]{2,1,0:T(2,128)S(1)}, f32[2,128]{1,0:T(2,128)S(1)}, f32[128,128]{1,0:T(8,128)S(1)}, ...), condition=%wide.region_28.0_spmd, body=%wide.region_26.28_spmd.sunk | while | flops 405012480 | bytes 3262025 | solution.py:71
  275.9 36.2 %all_to_all.31 = f32[32,128,128]{2,1,0:T(8,128)S(1)} all-to-all(f32[32,128,128]{2,1,0:T(8,128)} %bitcast.42), channel_id=1, replica_groups=mesh['loc_0'=4,'loc_1'=4,'loc_2'=2,'tm'=8] {'loc_0','loc_1','loc_2'}, dimensions={0} | all-to-all | bytes 4194304 | tf_op jit(solution)/shard_map/all_to_all | solution.py:47
  (61 shorter events, 34.1 us)
Async XLA Ops:
  2.4 27.0 %all-to-all-start = ((f32[8,128,128]{1,2,0:T(8,128)}), f32[8,128,128]{1,2,0:T(8,128)S(1)}, u32[]{:S(2)}, u32[]{:S(2)}) async-start(f32[8,128,128]{1,2,0:T(8,128)} %broadcast_in_dim.41), calls=%async_computation | async-start | bytes 1048576 | tf_op jit(solution)/shard_map/all_to_all | solution.py:19
  32.9 7.7 %copy-start.1 = (f32[2,4096]{1,0:T(2,128)S(1)}, f32[2,4096]{1,0:T(2,128)}, u32[]{:S(2)}) copy-start(f32[2,4096]{1,0:T(2,128)} %param.15) | copy-start | bytes 98308
  32.9 36.3 %all-to-all-start.1 = ((f32[32,128,128]{2,1,0:T(8,128)}), f32[32,128,128]{2,1,0:T(8,128)S(1)}, u32[]{:S(2)}, u32[]{:S(2)}) async-start(f32[32,128,128]{2,1,0:T(8,128)} %broadcast_in_dim.42), calls=%async_computation.1 | async-start | bytes 4194304 | tf_op jit(solution)/shard_map/all_to_all | solution.py:19
  69.2 3.8 %copy-start = (s32[128,128]{1,0:T(8,128)S(1)}, s32[128,128]{1,0:T(8,128)}, u32[]{:S(2)}) copy-start(s32[128,128]{1,0:T(8,128)} %param.14) | copy-start | bytes 196612
  69.2 3.8 %copy-start.5 = (f32[128]{0:T(128)S(1)}, f32[128]{0:T(128)}, u32[]{:S(2)}) copy-start(f32[128]{0:T(128)} %param.17) | copy-start | bytes 1540
  73.0 92.9 %copy-start.6 = (f32[1024]{0:T(1024)S(1)}, f32[1024]{0:T(1024)}, u32[]{:S(2)}) copy-start(f32[1024]{0:T(1024)} %param.16) | copy-start | bytes 12292
  168.8 37.5 %all-to-all-start.3 = ((f32[32,128,128]{2,1,0:T(8,128)}), f32[32,128,128]{2,1,0:T(8,128)S(1)}, u32[]{:S(2)}, u32[]{:S(2)}) async-start(f32[32,128,128]{2,1,0:T(8,128)} %broadcast_in_dim.44), calls=%async_computation.3 | async-start | bytes 4194304 | tf_op jit(solution)/shard_map/all_to_all | solution.py:19
  210.0 41.4 %copy-start.3 = (f32[2,4096]{1,0:T(2,128)S(1)}, f32[2,4096]{1,0:T(2,128)}, u32[]{:S(2)}) copy-start(f32[2,4096]{1,0:T(2,128)} %param.18) | copy-start | bytes 98308
  210.7 41.3 %copy-start.4 = (s32[4096]{0:T(1024)S(1)}, s32[4096]{0:T(1024)}, u32[]{:S(2)}) copy-start(s32[4096]{0:T(1024)} %param.19) | copy-start | bytes 49156
  246.7 19.4 %copy-start.2 = (f32[128,128]{1,0:T(8,128)}, f32[128,128]{1,0:T(8,128)S(1)}, u32[]{:S(2)}) copy-start(f32[128,128]{1,0:T(8,128)S(1)} %multiply_add_fusion) | copy-start | bytes 196612
  247.7 20.7 %all-to-all-start.4 = ((f32[8,128,128]{1,2,0:T(8,128)}), f32[8,128,128]{1,2,0:T(8,128)S(1)}, u32[]{:S(2)}, u32[]{:S(2)}) async-start(f32[8,128,128]{1,2,0:T(8,128)} %broadcast_in_dim.47), calls=%async_computation.4 | async-start | bytes 1048576 | tf_op jit(solution)/shard_map/all_to_all | solution.py:19
where the time goes:
time: 314 us; the launch traced here: 313 us
  blocking collectives  160 us (51%)
  waiting for transfers between devices  74 us (24%)
  starting transfers between devices  29.6 us (9%)
  local copies, waits for them, and re-layouts  22.9 us (7%)
  matrix products  15.4 us (5%)
  other arithmetic  6.18 us (2%)
  between operations  4.74 us (2%)
    psum x12, blocking collectives, by_axis(): shard = lax.psum(shard, axis)  107 us
    all_to_all x4, waiting for transfers between devices, from_everyone(): return lax.all_to_all(copies, axis, split_axis=0, concat_axis=0, tiled=True)  74 us
    all_to_all x1, blocking collectives, summed_on_arrival(): lax.all_to_all(parts, axis, split_axis=0, concat_axis=0, tiled=True)  36.2 us
    all_to_all x4, starting transfers between devices, from_everyone(): return lax.all_to_all(copies, axis, split_axis=0, concat_axis=0, tiled=True)  29.6 us
    all_to_all x1, blocking collectives, from_everyone(): return lax.all_to_all(copies, axis, split_axis=0, concat_axis=0, tiled=True)  16.1 us
    gather x1, local copies, waits for them, and re-layouts, on_device(): unseen_site_positions = test_coords[:, site_order]  14.1 us
    dot_general x4, matrix products, add_block(): jnp.dot(kernel, rows_part, precision=lax.Precision.HIGHEST, preferred_ele...  6.34 us
  transfers between devices with their start and end apart: 4, of which 3 were waited for; matrix products, arithmetic and copies ran while one was open for 6% of the time, Pallas kernels for 0%

commit v1 on v0

--- a/solution.py
+++ b/solution.py
@@ -32,7 +32,7 @@
 
 def by_axis(shard, axes):
     for axis in axes:
-        shard = lax.psum(shard, axis)
+        shard = jnp.sum(lax.all_gather(shard, axis), axis=0)
     return shard
 
 

time: 314 us -> 341 us (1.086)
  local copies, waits for them, and re-layouts: 22.9 us -> 47.4 us
  other arithmetic: 6.18 us -> 16.5 us
  blocking collectives: 160 us -> 152 us
    psum x12 -> x0, blocking collectives: 107 us -> none  [by_axis(): shard = lax.psum(shard, axis)]
    unnamed x0 -> x12, blocking collectives: none -> 99.4 us
    unnamed x15 -> x59, local copies, waits for them, and re-layouts: 0.68 us -> 25.2 us
    reduce_sum x0 -> x16, other arithmetic: none -> 10.2 us  [by_axis(): shard = jnp.sum(lax.all_gather(shard, axis), axis=0)]
  transfers between devices with their start and end apart: 4 -> 4, of which waited for: 3 -> 3; matrix products, arithmetic and copies ran while one was open for 6% -> 5% of each run, Pallas kernels for 0% -> 0%
where the time goes in v1:
time: 341 us; the launch traced here: 339 us
  blocking collectives  152 us (45%)
  waiting for transfers between devices  73.5 us (22%)
  local copies, waits for them, and re-layouts  47.4 us (14%)
  starting transfers between devices  29.6 us (9%)
  other arithmetic  16.5 us (5%)
  matrix products  15.5 us (5%)
  between operations  4.89 us (1%)
    unnamed x12, blocking collectives  99.4 us
    all_to_all x4, waiting for transfers between devices, from_everyone(): return lax.all_to_all(copies, axis, split_axis=0, concat_axis=0, tiled=True)  73.5 us
    all_to_all x1, blocking collectives, summed_on_arrival(): lax.all_to_all(parts, axis, split_axis=0, concat_axis=0, tiled=True)  36.2 us
    all_to_all x4, starting transfers between devices, from_everyone(): return lax.all_to_all(copies, axis, split_axis=0, concat_axis=0, tiled=True)  29.6 us
    unnamed x59, local copies, waits for them, and re-layouts  25.2 us
    all_to_all x1, blocking collectives, from_everyone(): return lax.all_to_all(copies, axis, split_axis=0, concat_axis=0, tiled=True)  16.1 us
    gather x1, local copies, waits for them, and re-layouts, on_device(): unseen_site_positions = test_coords[:, site_order]  14.1 us
    reduce_sum x16, other arithmetic, by_axis(): shard = jnp.sum(lax.all_gather(shard, axis), axis=0)  10.2 us
  transfers between devices with their start and end apart: 4, of which 3 were waited for; matrix products, arithmetic and copies ran while one was open for 5% of the time, Pallas kernels for 0%

profile of v1, /device:TPU:1, one launch (start us, length us, event | category | flops | bytes accessed | tf_op | source)
XLA Modules:
  0.0 339.2 jit_solution(5609335534036393890)
XLA Ops:
  2.4 9.0 %all-to-all-start = ((f32[8,128,128]{1,2,0:T(8,128)}), f32[8,128,128]{1,2,0:T(8,128)S(1)}, u32[]{:S(2)}, u32[]{:S(2)}) async-start(f32[8,128,128]{1,2,0:T(8,128)} %broadcast_in_dim.41), calls=%async_computation | async-start | bytes 1048576 | tf_op jit(solution)/shard_map/all_to_all | solution.py:19
  12.2 17.2 %all-to-all-done = f32[8,128,128]{1,2,0:T(8,128)S(1)} async-done(((f32[8,128,128]{1,2,0:T(8,128)}), f32[8,128,128]{1,2,0:T(8,128)S(1)}, u32[]{:S(2)}, u32[]{:S(2)}) %all-to-all-start) | async-done | bytes 524320 | tf_op jit(solution)/shard_map/all_to_all | solution.py:19
  32.9 7.7 %all-to-all-start.1 = ((f32[32,128,128]{2,1,0:T(8,128)}), f32[32,128,128]{2,1,0:T(8,128)S(1)}, u32[]{:S(2)}, u32[]{:S(2)}) async-start(f32[32,128,128]{2,1,0:T(8,128)} %broadcast_in_dim.42), calls=%async_computation.1 | async-start | bytes 4194304 | tf_op jit(solution)/shard_map/all_to_all | solution.py:19
  41.3 28.0 %all-to-all-done.1 = f32[32,128,128]{2,1,0:T(8,128)S(1)} async-done(((f32[32,128,128]{2,1,0:T(8,128)}), f32[32,128,128]{2,1,0:T(8,128)S(1)}, u32[]{:S(2)}, u32[]{:S(2)}) %all-to-all-start.1) | async-done | bytes 2097184 | tf_op jit(solution)/shard_map/all_to_all | solution.py:19
  69.3 3.8 %while.39 = (s32[]{:T(128)}, f32[128,128]{1,0:T(8,128)S(1)}, f32[2,128]{1,0:T(2,128)S(1)}, f32[2,4096]{1,0:T(2,128)S(1)}, f32[4096,128]{1,0:T(8,128)S(1)}, /*index=5*/s32[]{:T(128)}, s32[]{:T(128)}, s32[]{:T(128)}, s32[]{:T(128)}) while((s32[]{:T(128)}, f32[128,128]{1,0:T(8,128)S(1)}, f32[2,128]{1,0:T(2,128)S(1)}, ...), condition=%wide.region_7.8_spmd.clone, body=%wide.region_5.7_spmd.clone.sunk | while | flops 405045248 | bytes 3327133 | solution.py:89
  77.2 6.0 %all-reduce.18 = (f32[4]{0:T(128)S(1)}, f32[4]{0:T(128)S(1)}) all-reduce(f32[4]{0:T(128)S(1)} %dynamic-update-slice, f32[4]{0:T(128)S(1)} %dynamic-update-slice.4), channel_id=1, replica_groups=mesh['loc_0'=4,'loc_1'=4,'loc_2'=2,'tm'=8] {'loc_0'}, use_global_device_ids=true, to_apply=%add | all-reduce | flops 8 | bytes 64
  87.8 9.2 %all-reduce.17 = (f32[4]{0:T(128)S(1)}, f32[4]{0:T(128)S(1)}) all-reduce(f32[4]{0:T(128)S(1)} %dynamic-update-slice.1, f32[4]{0:T(128)S(1)} %dynamic-update-slice.5), channel_id=1, replica_groups=mesh['loc_0'=4,'loc_1'=4,'loc_2'=2,'tm'=8] {'loc_1'}, use_global_device_ids=true, to_apply=%add.1 | all-reduce | flops 8 | bytes 64
  101.6 5.2 %all-reduce.19 = (f32[2]{0:T(128)S(1)}, f32[2]{0:T(128)S(1)}) all-reduce(f32[2]{0:T(128)S(1)} %dynamic-update-slice.2, f32[2]{0:T(128)S(1)} %dynamic-update-slice.6), channel_id=1, replica_groups=mesh['loc_0'=4,'loc_1'=4,'loc_2'=2,'tm'=8] {'loc_2'}, use_global_device_ids=true, to_apply=%add.2 | all-reduce | flops 4 | bytes 32
  110.8 10.9 %all-reduce.16 = (f32[8]{0:T(128)S(1)}, f32[8]{0:T(128)S(1)}) all-reduce(f32[8]{0:T(128)S(1)} %dynamic-update-slice.3, f32[8]{0:T(128)S(1)} %dynamic-update-slice.7), channel_id=1, replica_groups=mesh['loc_0'=4,'loc_1'=4,'loc_2'=2,'tm'=8] {'tm'}, use_global_device_ids=true, to_apply=%add.3 | all-reduce | flops 16 | bytes 128
  126.5 6.5 %all-reduce.8 = f32[4]{0:T(128)S(1)} all-reduce(f32[4]{0:T(128)S(1)} %dynamic-update-slice.8), channel_id=1, replica_groups=mesh['loc_0'=4,'loc_1'=4,'loc_2'=2,'tm'=8] {'loc_0'}, use_global_device_ids=true, to_apply=%add.8 | all-reduce | flops 4 | bytes 32
  135.1 7.7 %all-reduce.9 = f32[4]{0:T(128)S(1)} all-reduce(f32[4]{0:T(128)S(1)} %dynamic-update-slice.9), channel_id=1, replica_groups=mesh['loc_0'=4,'loc_1'=4,'loc_2'=2,'tm'=8] {'loc_1'}, use_global_device_ids=true, to_apply=%add.9 | all-reduce | flops 4 | bytes 32
  144.9 10.2 %all-reduce.10 = f32[2]{0:T(128)S(1)} all-reduce(f32[2]{0:T(128)S(1)} %dynamic-update-slice.10), channel_id=1, replica_groups=mesh['loc_0'=4,'loc_1'=4,'loc_2'=2,'tm'=8] {'loc_2'}, use_global_device_ids=true, to_apply=%add.10 | all-reduce | flops 2 | bytes 16
  157.2 11.8 %all-reduce.11 = f32[8]{0:T(128)S(1)} all-reduce(f32[8]{0:T(128)S(1)} %dynamic-update-slice.11), channel_id=1, replica_groups=mesh['loc_0'=4,'loc_1'=4,'loc_2'=2,'tm'=8] {'tm'}, use_global_device_ids=true, to_apply=%add.11 | all-reduce | flops 8 | bytes 64
  171.2 16.1 %all_to_all.30 = f32[8,128,128]{1,2,0:T(8,128)S(1)} all-to-all(f32[8,128,128]{1,2,0:T(8,128)S(1)} %broadcast_in_dim.43), channel_id=1, replica_groups=mesh['loc_0'=4,'loc_1'=4,'loc_2'=2,'tm'=8] {'tm'}, dimensions={0} | all-to-all | bytes 1048576 | tf_op jit(solution)/shard_map/all_to_all | solution.py:19
  190.1 9.2 %all-to-all-start.3 = ((f32[32,128,128]{2,1,0:T(8,128)}), f32[32,128,128]{2,1,0:T(8,128)S(1)}, u32[]{:S(2)}, u32[]{:S(2)}) async-start(f32[32,128,128]{2,1,0:T(8,128)} %broadcast_in_dim.44), calls=%async_computation.3 | async-start | bytes 4194304 | tf_op jit(solution)/shard_map/all_to_all | solution.py:19
  199.3 28.3 %all-to-all-done.3 = f32[32,128,128]{2,1,0:T(8,128)S(1)} async-done(((f32[32,128,128]{2,1,0:T(8,128)}), f32[32,128,128]{2,1,0:T(8,128)S(1)}, u32[]{:S(2)}, u32[]{:S(2)}) %all-to-all-start.3) | async-done | bytes 2097184 | tf_op jit(solution)/shard_map/all_to_all | solution.py:19
  227.6 3.7 %while.40 = (s32[]{:T(128)}, f32[128,128]{1,0:T(8,128)S(1)}, f32[2,128]{1,0:T(2,128)S(1)}, f32[2,4096]{1,0:T(2,128)S(1)}, f32[4096,128]{1,0:T(8,128)S(1)}, /*index=5*/s32[]{:T(128)}, s32[]{:T(128)}, s32[]{:T(128)}, s32[]{:T(128)}) while((s32[]{:T(128)}, f32[128,128]{1,0:T(8,128)S(1)}, f32[2,128]{1,0:T(2,128)S(1)}, ...), condition=%wide.region_20.21_spmd.clone, body=%wide.region_18.20_spmd.clone.sunk | while | flops 405045248 | bytes 3327133 | solution.py:89
  233.4 6.3 %all-reduce.12 = f32[4]{0:T(128)S(1)} all-reduce(f32[4]{0:T(128)S(1)} %dynamic-update-slice.12), channel_id=1, replica_groups=mesh['loc_0'=4,'loc_1'=4,'loc_2'=2,'tm'=8] {'loc_0'}, use_global_device_ids=true, to_apply=%add.12 | all-reduce | flops 4 | bytes 32
  241.8 9.3 %all-reduce.13 = f32[4]{0:T(128)S(1)} all-reduce(f32[4]{0:T(128)S(1)} %dynamic-update-slice.13), channel_id=1, replica_groups=mesh['loc_0'=4,'loc_1'=4,'loc_2'=2,'tm'=8] {'loc_1'}, use_global_device_ids=true, to_apply=%add.13 | all-reduce | flops 4 | bytes 32
  253.1 5.2 %all-reduce.14 = f32[2]{0:T(128)S(1)} all-reduce(f32[2]{0:T(128)S(1)} %dynamic-update-slice.14), channel_id=1, replica_groups=mesh['loc_0'=4,'loc_1'=4,'loc_2'=2,'tm'=8] {'loc_2'}, use_global_device_ids=true, to_apply=%add.14 | all-reduce | flops 2 | bytes 16
  260.2 10.9 %all-reduce.15 = f32[8]{0:T(128)S(1)} all-reduce(f32[8]{0:T(128)S(1)} %dynamic-update-slice.15), channel_id=1, replica_groups=mesh['loc_0'=4,'loc_1'=4,'loc_2'=2,'tm'=8] {'tm'}, use_global_device_ids=true, to_apply=%add.15 | all-reduce | flops 8 | bytes 64
  278.5 14.1 %gather_fusion = f32[4096,2]{1,0:T(8,128)} fusion(f32[2,4096]{0,1:T(8,128)S(1)} %copy.23, s32[4096]{0:T(1024)S(1)} %fusion.53), kind=kCustom, calls=%fused_computation | custom fusion | bytes 81920 | tf_op jit(solution)/shard_map/gather | solution.py:142
  296.0 6.2 %while.38 = (s32[]{:T(128)}, f32[2,2048,128]{2,1,0:T(8,128)}, f32[2,2,2048]{2,1,0:T(2,128)S(1)}, f32[2,128]{1,0:T(2,128)S(1)}, f32[128,128]{1,0:T(8,128)S(1)}, /*index=5*/s32[]{:T(128)}) while((s32[]{:T(128)}, f32[2,2048,128]{2,1,0:T(8,128)}, f32[2,2,2048]{2,1,0:T(2,128)S(1)}, f32[2,128]{1,0:T(2,128)S(1)}, f32[128,128]{1,0:T(8,128)S(1)}, ...), condition=%wide.region_28.0_spmd, body=%wide.region_26.28_spmd.sunk | while | flops 405012480 | bytes 3262025 | solution.py:71
  302.3 36.2 %all_to_all.31 = f32[32,128,128]{2,1,0:T(8,128)S(1)} all-to-all(f32[32,128,128]{2,1,0:T(8,128)} %bitcast.62), channel_id=1, replica_groups=mesh['loc_0'=4,'loc_1'=4,'loc_2'=2,'tm'=8] {'loc_0','loc_1','loc_2'}, dimensions={0} | all-to-all | bytes 4194304 | tf_op jit(solution)/shard_map/all_to_all | solution.py:47
  (121 shorter events, 69.0 us)
Async XLA Ops:
  2.4 27.0 %all-to-all-start = ((f32[8,128,128]{1,2,0:T(8,128)}), f32[8,128,128]{1,2,0:T(8,128)S(1)}, u32[]{:S(2)}, u32[]{:S(2)}) async-start(f32[8,128,128]{1,2,0:T(8,128)} %broadcast_in_dim.41), calls=%async_computation | async-start | bytes 1048576 | tf_op jit(solution)/shard_map/all_to_all | solution.py:19
  32.9 7.7 %copy-start.10 = (u32[256]{0:T(256)S(1)}, u32[256]{0:T(256)}, u32[]{:S(2)}) copy-start(u32[256]{0:T(256)} %constant.151) | copy-start | bytes 3076
  32.9 8.3 %copy-start.1 = (f32[2,4096]{1,0:T(2,128)S(1)}, f32[2,4096]{1,0:T(2,128)}, u32[]{:S(2)}) copy-start(f32[2,4096]{1,0:T(2,128)} %param.15) | copy-start | bytes 98308
  32.9 36.3 %all-to-all-start.1 = ((f32[32,128,128]{2,1,0:T(8,128)}), f32[32,128,128]{2,1,0:T(8,128)S(1)}, u32[]{:S(2)}, u32[]{:S(2)}) async-start(f32[32,128,128]{2,1,0:T(8,128)} %broadcast_in_dim.42), calls=%async_computation.1 | async-start | bytes 4194304 | tf_op jit(solution)/shard_map/all_to_all | solution.py:19
  69.2 3.8 %copy-start = (s32[128,128]{1,0:T(8,128)S(1)}, s32[128,128]{1,0:T(8,128)}, u32[]{:S(2)}) copy-start(s32[128,128]{1,0:T(8,128)} %param.14) | copy-start | bytes 196612
  69.2 3.8 %copy-start.5 = (f32[128]{0:T(128)S(1)}, f32[128]{0:T(128)}, u32[]{:S(2)}) copy-start(f32[128]{0:T(128)} %param.17) | copy-start | bytes 1540
  69.2 7.3 %copy-start.9 = (u32[256]{0:T(256)S(1)}, u32[256]{0:T(256)}, u32[]{:S(2)}) copy-start(u32[256]{0:T(256)} %constant.156) | copy-start | bytes 3076
  69.2 18.0 %copy-start.8 = (u32[256]{0:T(256)S(1)}, u32[256]{0:T(256)}, u32[]{:S(2)}) copy-start(u32[256]{0:T(256)} %constant.161) | copy-start | bytes 3076
  69.2 31.8 %copy-start.7 = (u32[256]{0:T(256)S(1)}, u32[256]{0:T(256)}, u32[]{:S(2)}) copy-start(u32[256]{0:T(256)} %constant.166) | copy-start | bytes 3076
  73.0 114.2 %copy-start.6 = (f32[1024]{0:T(1024)S(1)}, f32[1024]{0:T(1024)}, u32[]{:S(2)}) copy-start(f32[1024]{0:T(1024)} %param.16) | copy-start | bytes 12292
  190.1 37.5 %all-to-all-start.3 = ((f32[32,128,128]{2,1,0:T(8,128)}), f32[32,128,128]{2,1,0:T(8,128)S(1)}, u32[]{:S(2)}, u32[]{:S(2)}) async-start(f32[32,128,128]{2,1,0:T(8,128)} %broadcast_in_dim.44), calls=%async_computation.3 | async-start | bytes 4194304 | tf_op jit(solution)/shard_map/all_to_all | solution.py:19
  231.4 46.4 %copy-start.3 = (f32[2,4096]{1,0:T(2,128)S(1)}, f32[2,4096]{1,0:T(2,128)}, u32[]{:S(2)}) copy-start(f32[2,4096]{1,0:T(2,128)} %param.18) | copy-start | bytes 98308
  240.3 38.1 %copy-start.4 = (s32[4096]{0:T(1024)S(1)}, s32[4096]{0:T(1024)}, u32[]{:S(2)}) copy-start(s32[4096]{0:T(1024)} %param.19) | copy-start | bytes 49156
  273.1 19.4 %copy-start.2 = (f32[128,128]{1,0:T(8,128)}, f32[128,128]{1,0:T(8,128)S(1)}, u32[]{:S(2)}) copy-start(f32[128,128]{1,0:T(8,128)S(1)} %multiply_add_fusion) | copy-start | bytes 196612
  274.1 20.7 %all-to-all-start.4 = ((f32[8,128,128]{1,2,0:T(8,128)}), f32[8,128,128]{1,2,0:T(8,128)S(1)}, u32[]{:S(2)}, u32[]{:S(2)}) async-start(f32[8,128,128]{1,2,0:T(8,128)} %broadcast_in_dim.47), calls=%async_computation.4 | async-start | bytes 1048576 | tf_op jit(solution)/shard_map/all_to_all | solution.py:19
